TPU v7x, 1024 devices: a whole 4x8x16 slice. The times are simulated.
1024 devices in a mesh: pipe: 4 (over y_hi), dp: 32 (over y_lo, z), tensor: 8 (over x, core).
Axes of the slice: x: 4, y: 8 (y_hi: 4, y_lo: 2; y = y_hi * 2 + y_lo), z: 16, core: 2. Of those that a mesh axis runs over, the one named last changes fastest.
Arguments:
- saved: bfloat16 [4, 2, 2048, 1024], P('pipe', None, 'dp'), may hold values from -6 to 6
- top_grad: bfloat16 [2, 2048, 1024], P(None, 'dp'), may hold values from -6 to 6
- gain: bfloat16 [4, 1024], P('pipe', 'dp'), may hold values from 0.25 to 1.75
- w_query: bfloat16 [4, 1024, 1536], P('pipe', 'dp', 'tensor'), may hold values from -0.1875 to 0.1875
- w_latent: bfloat16 [4, 1024, 576], P('pipe', 'dp'), may hold values from -0.1875 to 0.1875
- compressed_gain: bfloat16 [4, 512], P('pipe', 'dp'), may hold values from 0.25 to 1.75
- expand_weight: bfloat16 [4, 512, 2048], P('pipe', 'dp', 'tensor'), may hold values from -0.25 to 0.25
- w_output: bfloat16 [4, 1024, 1024], P('pipe', 'tensor', 'dp'), may hold values from -0.1875 to 0.1875
Outputs:
- input_grad: bfloat16 [4, 2, 2048, 1024], P('pipe', None, ('dp', 'tensor'))
- grad_gain: float32 [4, 1024], P('pipe', 'dp')
- grad_query: float32 [4, 1024, 1536], P('pipe', 'dp', 'tensor')
- grad_latent: float32 [4, 1024, 576], P('pipe', 'dp')
- grad_latent_gain: float32 [4, 512], P('pipe', 'dp')
- grad_expand: float32 [4, 512, 2048], P('pipe', 'dp', 'tensor')
- grad_output: float32 [4, 1024, 1024], P('pipe', 'tensor', 'dp')
All inputs are finite; a program needn't handle non-finite values.
Results may differ from a plain program's by a relative error of at most 0.04.
Values may be sent and summed in bfloat16 or wider, within the bound.
A program may use at most 64 MiB of HBM per device.

v0:
```python
import jax
import jax.numpy as jnp
from jax import lax
from jax.sharding import PartitionSpec as P

NOPE = 128
ROPE = 64
VDIM = 128
COMPRESSED_RANK = 512


EPS = 1e-06


def side_by_side(arrays, axis, dim, along):
    columns = [a.reshape(*a.shape[:along], -1) for a in arrays]
    both = jnp.concatenate(columns, axis=along)
    filled, at, finished = (lax.all_gather(both, axis, axis=dim, tiled=True), 0, [])
    for a, column in zip(arrays, columns):
        piece = filled[..., at : at + column.shape[along]]
        finished.append(piece.reshape(*piece.shape[:along], *a.shape[along:]))
        at += column.shape[along]
    return tuple(finished)


def from_everyone(x, axis):
    length = lax.axis_size(axis)
    return lax.all_to_all(jnp.broadcast_to(x[None], (length, *x.shape)), axis, 0, 0, tiled=True)


def taken_together(x, axis):
    everything = from_everyone(x, axis)
    return jnp.sum(everything.astype(jnp.float32), axis=0)


def passed_along(value, axis, steps):
    count = lax.axis_size(axis)
    first, last = (max(0, -steps), min(count, count - steps))
    return lax.ppermute(value, axis, [(source, source + steps) for source in range(first, last)])


def split_up(x, dim, length):
    shape = x.shape
    blocks = x.reshape(*shape[:dim], length, shape[dim] // length, *shape[dim + 1 :])
    return jnp.moveaxis(blocks, dim, 0)


def sum_packed(arrays, axis, dims):
    length = lax.axis_size(axis)
    blocks = [split_up(a, dim, length) for a, dim in zip(arrays, dims)]
    lines = jnp.concatenate([b.reshape(length, -1) for b in blocks], axis=1)
    span = max(16, -(-lines.shape[1] // 1024) * 8)
    lines = jnp.pad(lines, ((0, 0), (0, span * 128 - lines.shape[1]))).reshape(-1, 128)
    ravelled, at, finished = (lax.psum_scatter(lines, axis, tiled=True).reshape(-1), 0, [])
    for b in blocks:
        part = b[0]
        finished.append(ravelled[at : at + part.size].reshape(part.shape))
        at += part.size
    return tuple(finished)


def root_mean_scale(values, scale):
    return values * lax.rsqrt(jnp.mean(values * values, axis=-1, keepdims=True) + EPS) * scale


def rotary_angles(values):
    length = values.shape[0]
    half = values.shape[-1] // 2
    freq = jnp.exp(-jnp.log(10000.0) * jnp.arange(half, dtype=jnp.float32) / half)
    angle = jnp.arange(length, dtype=jnp.float32)[:, None] * freq[None, :]
    cosine = jnp.cos(angle)[:, None, :]
    sine = jnp.sin(angle)[:, None, :]
    first = values[..., :half]
    second = values[..., half:]
    return jnp.concatenate(
        [first * cosine - second * sine, second * cosine + first * sine], axis=-1
    )


def branch(normed, w_q, w_lat, latent_norm_gain, w_exp, w_out):
    length = normed.shape[0]
    heads = w_q.shape[1] // (NOPE + ROPE)
    rounded = normed.astype(jnp.bfloat16)
    query = jnp.dot(rounded, w_q, preferred_element_type=jnp.float32).reshape(
        length, heads, NOPE + ROPE
    )
    latent_state = jnp.dot(rounded, w_lat, preferred_element_type=jnp.float32)
    compressed_state = root_mean_scale(latent_state[:, :COMPRESSED_RANK], latent_norm_gain).astype(
        jnp.bfloat16
    )
    rotary_key_part = rotary_angles(latent_state[:, None, COMPRESSED_RANK:])[:, 0, :]
    expanded = jnp.dot(compressed_state, w_exp, preferred_element_type=jnp.float32).reshape(
        length, heads, NOPE + VDIM
    )
    key_nope = expanded[:, :, :NOPE]
    values = expanded[:, :, NOPE:].astype(jnp.bfloat16)
    query_rope = rotary_angles(query[:, :, NOPE:])
    scores = jnp.einsum("qhd,khd->hqk", query[:, :, :NOPE], key_nope) + jnp.einsum(
        "qhd,kd->hqk", query_rope, rotary_key_part
    )
    scores = scores * (NOPE + ROPE) ** (-0.5)
    causal = jnp.arange(length)[:, None] >= jnp.arange(length)[None, :]
    scores = jnp.where(causal[None], scores, -1e30)
    weights = jax.nn.softmax(scores, axis=-1).astype(jnp.bfloat16)
    mixed = jnp.einsum("hqk,khd->qhd", weights.astype(jnp.float32), values.astype(jnp.float32))
    mixed = mixed.astype(jnp.bfloat16).reshape(length, heads * VDIM)
    return jnp.dot(mixed, w_out, preferred_element_type=jnp.float32)


def shards(saved, top_grad, gain, w_query, w_latent, compressed_gain, expand_weight, w_output):
    gathered = (
        *side_by_side((gain, w_query, w_latent), "dp", 1, 2),
        *side_by_side((compressed_gain, expand_weight), "dp", 1, 2),
        lax.all_gather(w_output, "dp", axis=2, tiled=True),
    )
    gain32 = gathered[0][0].astype(jnp.float32)
    query_all = gathered[1][0]
    latent_all = gathered[2][0]
    lgain32 = gathered[3][0].astype(jnp.float32)
    expand_all = gathered[4][0]
    output_all = gathered[5][0]
    sections = lax.axis_size("pipe")
    section_index = lax.axis_index("pipe")
    tensor_count = lax.axis_size("tensor")
    tensor_rank = lax.axis_index("tensor")
    micro_count = saved.shape[1]
    length = saved.shape[2]
    width = saved.shape[3]
    share = length // tensor_count

    def compute(normed, upstream):
        unused, pull = jax.vjp(
            lambda value: branch(value, query_all, latent_all, lgain32, expand_all, output_all),
            normed,
        )
        return pull(upstream.astype(jnp.float32))[0]

    def skip(normed, upstream):
        return jnp.zeros_like(normed)

    gain_total = jnp.zeros((width,), jnp.float32)
    results = jnp.zeros((micro_count, share, width), jnp.bfloat16)
    stored = jnp.zeros((micro_count, length, width), jnp.bfloat16)
    received = jnp.zeros((length, width), jnp.bfloat16)
    for tick in range(sections + micro_count - 1):
        micro = tick - (sections - 1 - section_index)
        active = jnp.logical_and(micro >= 0, micro < micro_count)
        picked = jnp.clip(micro, 0, micro_count - 1)
        x_rows = lax.dynamic_index_in_dim(saved[0], picked, 0, keepdims=False)
        top_rows = lax.dynamic_index_in_dim(top_grad, picked, 0, keepdims=False)
        arrived = received
        upstream = jnp.where(section_index == sections - 1, top_rows, arrived)
        x_float = x_rows.astype(jnp.float32)
        normed, norm_pull = jax.vjp(root_mean_scale, x_float, gain32)
        branch_grad = lax.cond(active, compute, skip, normed, upstream)
        d_normed = taken_together(branch_grad.astype(jnp.bfloat16), "tensor").astype(jnp.float32)
        dx_norm, d_gain = norm_pull(d_normed)
        dx = (upstream.astype(jnp.float32) + dx_norm).astype(jnp.bfloat16)
        gain_total = gain_total + jnp.where(active, d_gain, 0.0)
        mine = lax.dynamic_slice_in_dim(dx, tensor_rank * share, share, 0)
        chosen = (jnp.arange(micro_count) == micro)[:, None, None]
        results = jnp.where(chosen, mine[None], results)
        stored = jnp.where(chosen, upstream[None], stored)
        received = passed_along(dx, "pipe", -1)
    totals = (
        jnp.zeros(query_all.shape, jnp.float32),
        jnp.zeros(latent_all.shape, jnp.float32),
        jnp.zeros(lgain32.shape, jnp.float32),
        jnp.zeros(expand_all.shape, jnp.float32),
        jnp.zeros(output_all.shape, jnp.float32),
    )
    for micro_index in range(micro_count):
        normed_again = root_mean_scale(saved[0, micro_index].astype(jnp.float32), gain32)
        unused, weight_pull = jax.vjp(
            lambda w_q, w_lat, lat_gain, w_exp, w_out: branch(
                normed_again, w_q, w_lat, lat_gain, w_exp, w_out
            ),
            query_all,
            latent_all,
            lgain32,
            expand_all,
            output_all,
        )
        cotangents = weight_pull(stored[micro_index].astype(jnp.float32))
        totals = tuple(
            (total + piece.astype(jnp.float32) for total, piece in zip(totals, cotangents))
        )
    gain_part = jnp.where(tensor_rank == 0, gain_total, 0.0)
    grad_q, grad_lat, grad_lg, grad_e, grad_o = totals
    out_q, part_lat, part_lg, out_e, out_o, part_gain = tuple(
        (
            part.astype(jnp.float32)
            for part in sum_packed(
                (
                    grad_q.astype(jnp.bfloat16),
                    grad_lat.astype(jnp.bfloat16),
                    grad_lg.astype(jnp.bfloat16),
                    grad_e.astype(jnp.bfloat16),
                    grad_o.astype(jnp.bfloat16),
                    gain_part.astype(jnp.bfloat16),
                ),
                "dp",
                (0, 0, 0, 0, 1, 0),
            )
        )
    )
    out_lat, out_lg, out_gain = (
        taken_together(part_lat.astype(jnp.bfloat16), "tensor").astype(jnp.float32),
        taken_together(part_lg.astype(jnp.bfloat16), "tensor").astype(jnp.float32),
        taken_together(part_gain.astype(jnp.bfloat16), "tensor").astype(jnp.float32),
    )
    return (
        results[None],
        out_gain[None],
        out_q[None],
        out_lat[None],
        out_lg[None],
        out_e[None],
        out_o[None],
    )


def solution(mesh):
    in_specs = (
        P("pipe", None, "dp", None),
        P(None, "dp", None),
        P("pipe", "dp"),
        P("pipe", "dp", "tensor"),
        P("pipe", "dp", None),
        P("pipe", "dp"),
        P("pipe", "dp", "tensor"),
        P("pipe", "tensor", "dp"),
    )
    out_specs = (
        P("pipe", None, ("dp", "tensor"), None),
        P("pipe", "dp"),
        P("pipe", "dp", "tensor"),
        P("pipe", "dp", None),
        P("pipe", "dp"),
        P("pipe", "dp", "tensor"),
        P("pipe", "tensor", "dp"),
    )
    return jax.shard_map(shards, mesh=mesh, in_specs=in_specs, out_specs=out_specs, check_vma=False)
```

profile of v0, /device:TPU:1, one launch (start us, length us, event | category | flops | bytes accessed | tf_op | source)
XLA Modules:
  0.0 676.9 jit_solution(7732253873134248574)
XLA Ops:
  8.0 1.5 pad_maximum_fusion
  13.0 66.4 %all_gather.11 = bf16[1,512,257]{2,1,0:T(8,128)(2,1)S(1)} all-gather(bf16[1,16,257]{2,1,0:T(8,128)(2,1)S(1)} %pad_maximum_fusion.1), channel_id=1, replica_groups=mesh['pipe'=4,'dp'=32,'tensor'=8] {'dp'}, dimensions={1}, use_global_device_ids=true | all-gather | bytes 271392 | tf_op jit(solution)/shard_map/all_gather | solution.py:18
  79.6 49.2 %all_gather.9 = bf16[1,128,1024]{1,2,0:T(8,128)(2,1)S(1)} all-gather(bf16[1,128,32]{1,2,0:T(8,128)(2,1)} %param.25), channel_id=1, replica_groups=mesh['pipe'=4,'dp'=32,'tensor'=8] {'dp'}, dimensions={2}, use_global_device_ids=true | all-gather | bytes 270336 | tf_op jit(solution)/shard_map/all_gather | solution.py:114
  129.1 5.6 all-gather.2.cloned.1.call-done
  137.1 2.0 slice_bitcast_fusion.35
  140.3 27.4 %all-to-all-start = ((bf16[8,64,1024]{2,1,0:T(8,128)(2,1)}), bf16[8,64,1024]{2,1,0:T(8,128)(2,1)}, u32[]{:S(2)}, u32[]{:S(2)}) async-start(bf16[8,64,1024]{2,1,0:T(8,128)(2,1)} %broadcast_in_dim.477), calls=%async_computation | async-start | bytes 2097152 | tf_op jit(solution)/shard_map/all_to_all | solution.py:28
  170.4 12.4 %all-to-all-done = bf16[8,64,1024]{2,1,0:T(8,128)(2,1)} async-done(((bf16[8,64,1024]{2,1,0:T(8,128)(2,1)}), bf16[8,64,1024]{2,1,0:T(8,128)(2,1)}, u32[]{:S(2)}, u32[]{:S(2)}) %all-to-all-start) | async-done | bytes 1048608 | tf_op jit(solution)/shard_map/all_to_all | solution.py:28
  182.8 1.4 convert_reduce_fusion.4
  185.7 1.8 convert_multiply_fusion.18
  189.4 8.7 %collective-permute-done = bf16[64,1024]{1,0:T(8,128)(2,1)S(1)} collective-permute-done((bf16[64,1024]{1,0:T(8,128)(2,1)S(1)}, bf16[64,1024]{1,0:T(8,128)(2,1)S(1)}, u32[]{:S(2)}, u32[]{:S(2)}) %collective-permute-start) | collective-permute-done | bytes 131104 | tf_op jit(solution)/shard_map/ppermute | solution.py:39
  199.2 4.7 all-to-all-start.1
  204.0 2.2 fusion.388
  206.2 2.1 convolution_bitcast_fusion.40
  210.1 8.9 %all-to-all-done.1 = bf16[8,64,1024]{2,1,0:T(8,128)(2,1)} async-done(((bf16[8,64,1024]{2,1,0:T(8,128)(2,1)}), bf16[8,64,1024]{2,1,0:T(8,128)(2,1)}, u32[]{:S(2)}, u32[]{:S(2)}) %all-to-all-start.1) | async-done | bytes 1048608 | tf_op jit(solution)/shard_map/all_to_all | solution.py:28
  222.7 2.1 convolution_bitcast_fusion.42
  224.8 6.8 %collective-permute-done.1 = bf16[64,1024]{1,0:T(8,128)(2,1)S(1)} collective-permute-done((bf16[64,1024]{1,0:T(8,128)(2,1)S(1)}, bf16[64,1024]{1,0:T(8,128)(2,1)S(1)}, u32[]{:S(2)}, u32[]{:S(2)}) %collective-permute-start.1) | collective-permute-done | bytes 131104 | tf_op jit(solution)/shard_map/ppermute | solution.py:39
  233.0 2.0 broadcast_in_dim.481
  235.0 4.9 all-to-all-start.2
  239.9 1.6 multiply_subtract_fusion.11
  244.2 10.8 %all-to-all-done.2 = bf16[8,64,1024]{2,1,0:T(8,128)(2,1)} async-done(((bf16[8,64,1024]{2,1,0:T(8,128)(2,1)}), bf16[8,64,1024]{2,1,0:T(8,128)(2,1)}, u32[]{:S(2)}, u32[]{:S(2)}) %all-to-all-start.2) | async-done | bytes 1048608 | tf_op jit(solution)/shard_map/all_to_all | solution.py:28
  255.0 1.5 convert_reduce_fusion.2
  260.7 16.5 %collective-permute-done.2 = bf16[64,1024]{1,0:T(8,128)(2,1)S(1)} collective-permute-done((bf16[64,1024]{1,0:T(8,128)(2,1)S(1)}, bf16[64,1024]{1,0:T(8,128)(2,1)S(1)}, u32[]{:S(2)}, u32[]{:S(2)}) %collective-permute-start.2) | collective-permute-done | bytes 131104 | tf_op jit(solution)/shard_map/ppermute | solution.py:39
  278.0 6.9 %conditional.8 = (bf16[64,1024]{1,0:T(8,128)(2,1)}) conditional(s32[]{:T(128)} %convert_element_type.680, () %tuple.44, (bf16[64,1024]{1,0:T(8,128)(2,1)}, bf16[128,1024]{0,1:T(8,128)(2,1)S(1)}, f32[1024]{0:T(1024)S(1)}, f32[64,1024]{1,0:T(8,128)}, bf16[1024,576]{1,0:T(8,128)(2,1)S(1)}, /*index=5*/f32[512]{0:T(512)S(1)}, ...), branch_computations={%region_31.32_spmd, %region_32.38_spmd} | conditional | flops 259727776 | bytes 8170916 | solution.py:155
  284.8 2.0 broadcast_in_dim.483
  286.8 5.6 all-to-all-start.3
  296.5 11.0 %all-to-all-done.3 = bf16[8,64,1024]{2,1,0:T(8,128)(2,1)} async-done(((bf16[8,64,1024]{2,1,0:T(8,128)(2,1)}), bf16[8,64,1024]{2,1,0:T(8,128)(2,1)}, u32[]{:S(2)}, u32[]{:S(2)}) %all-to-all-start.3) | async-done | bytes 1048608 | tf_op jit(solution)/shard_map/all_to_all | solution.py:28
  307.6 1.5 convert_reduce_fusion.1
  311.9 1.4 collective-permute-start.3
  313.4 7.1 %collective-permute-done.3 = bf16[64,1024]{1,0:T(8,128)(2,1)S(1)} collective-permute-done((bf16[64,1024]{1,0:T(8,128)(2,1)S(1)}, bf16[64,1024]{1,0:T(8,128)(2,1)S(1)}, u32[]{:S(2)}, u32[]{:S(2)}) %collective-permute-start.3) | collective-permute-done | bytes 131104 | tf_op jit(solution)/shard_map/ppermute | solution.py:39
  329.6 1.7 multiply_add_fusion.38
  332.5 1.9 fusion.237
  334.4 2.0 copy.153
  336.4 2.4 reshape_reshape.9
  338.9 5.0 conditional.9
  343.8 2.0 broadcast_in_dim.485
  345.9 5.8 all-to-all-start.4
  353.9 1.6 reshape_reshape.10
  363.1 3.6 dynamic-update-slice.3
  366.7 3.4 dynamic-update-slice.4
  373.2 1.7 pad.257
  375.0 2.4 reshape.1676
  383.3 232.5 %all-reduce.74.cloned.1.call-done = bf16[8448,128]{1,0:T(8,128)(2,1)} async-done(((bf16[8448,128]{1,0:T(8,128)(2,1)}), bf16[8448,128]{1,0:T(8,128)(2,1)}) %all-reduce.74.cloned.1.call-update) | async-done | bytes 2162704
  617.3 26.7 %all-to-all-start.7 = ((bf16[8,1,16]{2,1,0:T(2,128)(2,1)}), bf16[8,1,16]{2,1,0:T(2,128)(2,1)S(1)}, u32[]{:S(2)}, u32[]{:S(2)}) async-start(bf16[8,1,16]{2,1,0:T(2,128)(2,1)} %broadcast_in_dim.525), calls=%async_computation.7 | async-start | bytes 8192 | tf_op jit(solution)/shard_map/all_to_all | solution.py:28
  644.1 4.4 all-to-all-done.7
  649.1 3.9 all-to-all-start.5
  653.9 3.7 all-to-all-done.5
  658.3 4.0 all-to-all-start.6
  666.1 3.3 all-to-all-done.6
  (430 shorter events, 84.9 us)
Async XLA Ops:
  7.2 121.6 %copy-start = (bf16[1,2,64,1024]{3,2,1,0:T(8,128)(2,1)S(1)}, bf16[1,2,64,1024]{3,2,1,0:T(8,128)(2,1)}, u32[]{:S(2)}) copy-start(bf16[1,2,64,1024]{3,2,1,0:T(8,128)(2,1)} %param.18) | copy-start | bytes 786436
  7.2 127.5 %all-gather.2.cloned.1.call-start = ((), (), s32[]{:S(2)}) async-start(), calls=%async_computation.8 | async-start | bytes 1892352 | tf_op jit(solution)/shard_map/all_gather | solution.py:18
  13.0 126.1 %copy-start.18 = (bf16[64,1024]{1,0:T(8,128)(2,1)}, bf16[64,1024]{1,0:T(8,128)(2,1)S(1)}, u32[]{:S(2)}) copy-start(bf16[64,1024]{1,0:T(8,128)(2,1)S(1)} %select_bitcast_fusion) | copy-start | bytes 393220
  128.8 55.4 %copy-start.86 = (f32[64]{0:T(128)}, f32[64]{0:T(128)S(1)}, u32[]{:S(2)}) copy-start(f32[64]{0:T(128)S(1)} %fusion.359) | copy-start | bytes 772
  140.3 42.5 %all-to-all-start = ((bf16[8,64,1024]{2,1,0:T(8,128)(2,1)}), bf16[8,64,1024]{2,1,0:T(8,128)(2,1)}, u32[]{:S(2)}, u32[]{:S(2)}) async-start(bf16[8,64,1024]{2,1,0:T(8,128)(2,1)} %broadcast_in_dim.477), calls=%async_computation | async-start | bytes 2097152 | tf_op jit(solution)/shard_map/all_to_all | solution.py:28
  167.7 17.9 %copy-start.3 = (bf16[2,64,1024]{2,1,0:T(8,128)(2,1)S(1)}, bf16[2,64,1024]{2,1,0:T(8,128)(2,1)}, u32[]{:S(2)}) copy-start(bf16[2,64,1024]{2,1,0:T(8,128)(2,1)} %param.19) | copy-start | bytes 786436
  185.1 13.0 %copy-start.104 = (f32[64]{0:T(128)}, f32[64]{0:T(128)S(1)}, u32[]{:S(2)}) copy-start(f32[64]{0:T(128)S(1)} %get-tuple-element.362) | copy-start | bytes 772
  185.1 13.0 %copy-start.105 = (f32[64]{0:T(128)}, f32[64]{0:T(128)S(1)}, u32[]{:S(2)}) copy-start(f32[64]{0:T(128)S(1)} %get-tuple-element.363) | copy-start | bytes 772
  185.1 13.0 %copy-start.99 = (f32[64]{0:T(128)}, f32[64]{0:T(128)S(1)}, u32[]{:S(2)}) copy-start(f32[64]{0:T(128)S(1)} %fusion.363) | copy-start | bytes 772
  185.6 12.4 %copy-start.79 = (f32[64]{0:T(128)}, f32[64]{0:T(128)S(1)}, u32[]{:S(2)}) copy-start(f32[64]{0:T(128)S(1)} %get-tuple-element.511) | copy-start | bytes 772
  187.5 10.5 %collective-permute-start = (bf16[64,1024]{1,0:T(8,128)(2,1)S(1)}, bf16[64,1024]{1,0:T(8,128)(2,1)S(1)}, u32[]{:S(2)}, u32[]{:S(2)}) collective-permute-start(bf16[64,1024]{1,0:T(8,128)(2,1)S(1)} %get-tuple-element.459), channel_id=1, source_target_pairs={{256,0},{512,256},{768,512},{257,1},{513,257},{769,513},{258,2},{5... | collective-permute-start | bytes 393224 | tf_op jit(solution)/shard_map/ppermute | solution.py:39
  199.2 19.8 %all-to-all-start.1 = ((bf16[8,64,1024]{2,1,0:T(8,128)(2,1)}), bf16[8,64,1024]{2,1,0:T(8,128)(2,1)}, u32[]{:S(2)}, u32[]{:S(2)}) async-start(bf16[8,64,1024]{2,1,0:T(8,128)(2,1)} %broadcast_in_dim.479), calls=%async_computation.1 | async-start | bytes 2097152 | tf_op jit(solution)/shard_map/all_to_all | solution.py:28
  209.5 11.7 %copy-start.103 = (f32[64]{0:T(128)S(1)}, f32[64]{0:T(128)}, u32[]{:S(2)}) copy-start(f32[64]{0:T(128)} %copy-done.102) | copy-start | bytes 772
  220.5 11.1 %copy-start.4 = (bf16[2,64,1024]{2,1,0:T(8,128)(2,1)S(1)}, bf16[2,64,1024]{2,1,0:T(8,128)(2,1)}, u32[]{:S(2)}) copy-start(bf16[2,64,1024]{2,1,0:T(8,128)(2,1)} %param.19) | copy-start | bytes 786436
  221.4 10.9 %copy-start.36 = (bf16[64,1024]{1,0:T(8,128)(2,1)}, bf16[64,1024]{1,0:T(8,128)(2,1)S(1)}, u32[]{:S(2)}) copy-start(bf16[64,1024]{1,0:T(8,128)(2,1)S(1)} %fusion.280) | copy-start | bytes 393220
  221.4 10.2 %collective-permute-start.1 = (bf16[64,1024]{1,0:T(8,128)(2,1)S(1)}, bf16[64,1024]{1,0:T(8,128)(2,1)S(1)}, u32[]{:S(2)}, u32[]{:S(2)}) collective-permute-start(bf16[64,1024]{1,0:T(8,128)(2,1)S(1)} %fusion.280), channel_id=1, source_target_pairs={{256,0},{512,256},{768,512},{257,1},{513,257},{769,513},{258,2},{5... | collective-permute-start | bytes 393224 | tf_op jit(solution)/shard_map/ppermute | solution.py:39
  235.0 20.0 %all-to-all-start.2 = ((bf16[8,64,1024]{2,1,0:T(8,128)(2,1)}), bf16[8,64,1024]{2,1,0:T(8,128)(2,1)}, u32[]{:S(2)}, u32[]{:S(2)}) async-start(bf16[8,64,1024]{2,1,0:T(8,128)(2,1)} %broadcast_in_dim.481), calls=%async_computation.2 | async-start | bytes 2097152 | tf_op jit(solution)/shard_map/all_to_all | solution.py:28
  243.2 17.4 %copy-start.21 = (bf16[64,1,256]{2,0,1:T(8,128)(2,1)}, bf16[64,1,256]{2,0,1:T(8,128)(2,1)S(1)}, u32[]{:S(2)}) copy-start(bf16[64,1,256]{2,0,1:T(8,128)(2,1)S(1)} %convolution_bitcast_fusion.41) | copy-start | bytes 98308
  244.2 77.3 %copy-start.67 = (f32[64]{0:T(128)}, f32[64]{0:T(128)S(1)}, u32[]{:S(2)}) copy-start(f32[64]{0:T(128)S(1)} %get-tuple-element.501) | copy-start | bytes 772
  255.0 22.3 %copy-start.5 = (bf16[2,64,1024]{2,1,0:T(8,128)(2,1)S(1)}, bf16[2,64,1024]{2,1,0:T(8,128)(2,1)}, u32[]{:S(2)}) copy-start(bf16[2,64,1024]{2,1,0:T(8,128)(2,1)} %param.19) | copy-start | bytes 786436
  258.0 20.0 %copy-start.37 = (bf16[64,1024]{1,0:T(8,128)(2,1)}, bf16[64,1024]{1,0:T(8,128)(2,1)S(1)}, u32[]{:S(2)}) copy-start(bf16[64,1024]{1,0:T(8,128)(2,1)S(1)} %fusion.282) | copy-start | bytes 393220
  258.0 19.3 %collective-permute-start.2 = (bf16[64,1024]{1,0:T(8,128)(2,1)S(1)}, bf16[64,1024]{1,0:T(8,128)(2,1)S(1)}, u32[]{:S(2)}, u32[]{:S(2)}) collective-permute-start(bf16[64,1024]{1,0:T(8,128)(2,1)S(1)} %fusion.282), channel_id=1, source_target_pairs={{256,0},{512,256},{768,512},{257,1},{513,257},{769,513},{258,2},{5... | collective-permute-start | bytes 393224 | tf_op jit(solution)/shard_map/ppermute | solution.py:39
  260.7 31.7 %copy-start.110 = (f32[64]{0:T(128)}, f32[64]{0:T(128)S(1)}, u32[]{:S(2)}) copy-start(f32[64]{0:T(128)S(1)} %multiply_reduce_fusion.22) | copy-start | bytes 772
  286.8 20.7 %all-to-all-start.3 = ((bf16[8,64,1024]{2,1,0:T(8,128)(2,1)}), bf16[8,64,1024]{2,1,0:T(8,128)(2,1)}, u32[]{:S(2)}, u32[]{:S(2)}) async-start(bf16[8,64,1024]{2,1,0:T(8,128)(2,1)} %broadcast_in_dim.483), calls=%async_computation.3 | async-start | bytes 2097152 | tf_op jit(solution)/shard_map/all_to_all | solution.py:28
  294.8 29.6 %copy-start.69 = (f32[64]{0:T(128)}, f32[64]{0:T(128)S(1)}, u32[]{:S(2)}) copy-start(f32[64]{0:T(128)S(1)} %get-tuple-element.497) | copy-start | bytes 772
  307.5 12.9 %copy-start.6 = (bf16[2,64,1024]{2,1,0:T(8,128)(2,1)S(1)}, bf16[2,64,1024]{2,1,0:T(8,128)(2,1)}, u32[]{:S(2)}) copy-start(bf16[2,64,1024]{2,1,0:T(8,128)(2,1)} %param.19) | copy-start | bytes 786436
  307.5 13.0 %copy-start.14 = (bf16[64,1024]{1,0:T(8,128)(2,1)S(1)}, bf16[64,1024]{1,0:T(8,128)(2,1)}, u32[]{:S(2)}) copy-start(bf16[64,1024]{1,0:T(8,128)(2,1)} %bitcast_select_fusion.1) | copy-start | bytes 393220
  307.5 13.0 %copy-start.19 = (bf16[64,1024]{1,0:T(8,128)(2,1)S(1)}, bf16[64,1024]{1,0:T(8,128)(2,1)}, u32[]{:S(2)}) copy-start(bf16[64,1024]{1,0:T(8,128)(2,1)} %copy-done.18) | copy-start | bytes 393220
  307.5 13.0 %copy-start.87 = (pred[2]{0:T(512)(128)(4,1)S(1)}, pred[2]{0:T(512)(128)(4,1)}, u32[]{:S(2)}) copy-start(pred[2]{0:T(512)(128)(4,1)} %get-tuple-element.512) | copy-start | bytes 10
  307.5 13.0 %copy-start.89 = (pred[2]{0:T(512)(128)(4,1)S(1)}, pred[2]{0:T(512)(128)(4,1)}, u32[]{:S(2)}) copy-start(pred[2]{0:T(512)(128)(4,1)} %get-tuple-element.513) | copy-start | bytes 10
  307.5 13.0 %copy-start.93 = (pred[2]{0:T(512)(128)(4,1)S(1)}, pred[2]{0:T(512)(128)(4,1)}, u32[]{:S(2)}) copy-start(pred[2]{0:T(512)(128)(4,1)} %iota_compare_fusion.10) | copy-start | bytes 10
  307.5 13.0 %copy-start.95 = (pred[2]{0:T(512)(128)(4,1)S(1)}, pred[2]{0:T(512)(128)(4,1)}, u32[]{:S(2)}) copy-start(pred[2]{0:T(512)(128)(4,1)} %iota_compare_fusion.7) | copy-start | bytes 10
  307.6 13.0 %copy-start.97 = (pred[2]{0:T(512)(128)(4,1)S(1)}, pred[2]{0:T(512)(128)(4,1)}, u32[]{:S(2)}) copy-start(pred[2]{0:T(512)(128)(4,1)} %iota_compare_fusion.6) | copy-start | bytes 10
  311.1 10.1 %copy-start.84 = (f32[64]{0:T(128)S(1)}, f32[64]{0:T(128)}, u32[]{:S(2)}) copy-start(f32[64]{0:T(128)} %fusion.344) | copy-start | bytes 772
  311.1 10.2 %copy-start.22 = (bf16[64,1,256]{2,0,1:T(8,128)(2,1)S(1)}, bf16[64,1,256]{2,0,1:T(8,128)(2,1)}, u32[]{:S(2)}) copy-start(bf16[64,1,256]{2,0,1:T(8,128)(2,1)} %copy-done.21) | copy-start | bytes 98308
  311.1 10.2 %copy-start.114 = (f32[64]{0:T(128)S(1)}, f32[64]{0:T(128)}, u32[]{:S(2)}) copy-start(f32[64]{0:T(128)} %multiply_divide_fusion.5) | copy-start | bytes 772
  311.9 9.7 %copy-start.33 = (f32[64,1,192]{2,0,1:T(8,128)S(1)}, f32[64,1,192]{2,0,1:T(8,128)}, u32[]{:S(2)}) copy-start(f32[64,1,192]{2,0,1:T(8,128)} %convolution_bitcast_fusion.40) | copy-start | bytes 147460
  311.9 9.8 %copy-start.52 = (bf16[64,1,32]{2,0,1:T(8,128)(2,1)S(1)}, bf16[64,1,32]{2,0,1:T(8,128)(2,1)}, u32[]{:S(2)}) copy-start(bf16[64,1,32]{2,0,1:T(8,128)(2,1)} %copy-done.51) | copy-start | bytes 12292
  311.9 9.8 %copy-start.54 = (bf16[64,1,32]{2,0,1:T(8,128)(2,1)S(1)}, bf16[64,1,32]{2,0,1:T(8,128)(2,1)}, u32[]{:S(2)}) copy-start(bf16[64,1,32]{2,0,1:T(8,128)(2,1)} %copy-done.53) | copy-start | bytes 12292
  311.9 8.5 %collective-permute-start.3 = (bf16[64,1024]{1,0:T(8,128)(2,1)S(1)}, bf16[64,1024]{1,0:T(8,128)(2,1)S(1)}, u32[]{:S(2)}, u32[]{:S(2)}) collective-permute-start(bf16[64,1024]{1,0:T(8,128)(2,1)S(1)} %fusion.284), channel_id=1, source_target_pairs={{256,0},{512,256},{768,512},{257,1},{513,257},{769,513},{258,2},{5... | collective-permute-start | bytes 393224 | tf_op jit(solution)/shard_map/ppermute | solution.py:39
  313.4 9.2 %copy-start.48 = (bf16[64,1,32]{2,0,1:T(8,128)(2,1)S(1)}, bf16[64,1,32]{2,0,1:T(8,128)(2,1)}, u32[]{:S(2)}) copy-start(bf16[64,1,32]{2,0,1:T(8,128)(2,1)} %copy-done.47) | copy-start | bytes 12292
  313.4 9.2 %copy-start.50 = (bf16[64,1,32]{2,0,1:T(8,128)(2,1)S(1)}, bf16[64,1,32]{2,0,1:T(8,128)(2,1)}, u32[]{:S(2)}) copy-start(bf16[64,1,32]{2,0,1:T(8,128)(2,1)} %copy-done.49) | copy-start | bytes 12292
  345.9 24.2 %all-to-all-start.4 = ((bf16[8,64,1024]{2,1,0:T(8,128)(2,1)}), bf16[8,64,1024]{2,1,0:T(8,128)(2,1)}, u32[]{:S(2)}, u32[]{:S(2)}) async-start(bf16[8,64,1024]{2,1,0:T(8,128)(2,1)} %broadcast_in_dim.485), calls=%async_computation.4 | async-start | bytes 2097152 | tf_op jit(solution)/shard_map/all_to_all | solution.py:28
  351.7 264.1 %all-reduce.74.cloned.1.call-start = ((), (), s32[]{:S(2)}) async-start(), calls=%async_computation.9 | async-start | bytes 4325376
  361.7 9.8 %copy-start.100 = (f32[64]{0:T(128)S(1)}, f32[64]{0:T(128)}, u32[]{:S(2)}) copy-start(f32[64]{0:T(128)} %copy-done.99) | copy-start | bytes 772
  617.3 31.2 %all-to-all-start.7 = ((bf16[8,1,16]{2,1,0:T(2,128)(2,1)}), bf16[8,1,16]{2,1,0:T(2,128)(2,1)S(1)}, u32[]{:S(2)}, u32[]{:S(2)}) async-start(bf16[8,1,16]{2,1,0:T(2,128)(2,1)} %broadcast_in_dim.525), calls=%async_computation.7 | async-start | bytes 8192 | tf_op jit(solution)/shard_map/all_to_all | solution.py:28
  649.1 8.5 %all-to-all-start.5 = ((bf16[8,1,32]{2,1,0:T(2,128)(2,1)}), bf16[8,1,32]{2,1,0:T(2,128)(2,1)S(1)}, u32[]{:S(2)}, u32[]{:S(2)}) async-start(bf16[8,1,32]{2,1,0:T(2,128)(2,1)} %broadcast_in_dim.520), calls=%async_computation.5 | async-start | bytes 8192 | tf_op jit(solution)/shard_map/all_to_all | solution.py:28
  658.3 11.1 %all-to-all-start.6 = ((bf16[8,32,576]{2,1,0:T(8,128)(2,1)}), bf16[8,32,576]{2,1,0:T(8,128)(2,1)S(1)}, u32[]{:S(2)}, u32[]{:S(2)}) async-start(bf16[8,32,576]{2,1,0:T(8,128)(2,1)} %broadcast_in_dim.523), calls=%async_computation.6 | async-start | bytes 655360 | tf_op jit(solution)/shard_map/all_to_all | solution.py:28
  (79 other events, 307.6 us)
Sparse Core Ops, SparseCore 0:
  11.2 123.3 all-gather.1
  377.5 238.2 all-reduce.73
where the time goes:
time: 680 us; the launch traced here: 677 us
  waiting for transfers between devices  332 us (49%)
  blocking collectives  116 us (17%)
  starting transfers between devices  88.3 us (13%)
  local copies, waits for them, and re-layouts  53.7 us (8%)
  other arithmetic  37.8 us (6%)
  matrix products  33.3 us (5%)
  between operations  16.2 us (2%)
    unnamed x3, waiting for transfers between devices  233 us
    all_to_all x8, starting transfers between devices, from_everyone(): lax.all_to_all(jnp.broadcast_to(x[None], (length, *x.shape)), axis, 0, 0,...  83 us
    all_gather x1, blocking collectives, side_by_side(): lax.all_gather(both, axis, axis=dim, tiled=True)  66.4 us
    all_to_all x8, waiting for transfers between devices, from_everyone(): lax.all_to_all(jnp.broadcast_to(x[None], (length, *x.shape)), axis, 0, 0,...  54.4 us
    all_gather x1, blocking collectives, shards(): lax.all_gather(w_output, 'dp', axis=2, tiled=True)  49.2 us
    ppermute x4, waiting for transfers between devices, passed_along(): lax.ppermute(value, axis, [(source, source + steps) for source in range(f...  39.1 us
    unnamed x231, local copies, waits for them, and re-layouts  16 us
  transfers between devices with their start and end apart: 14, of which 13 were waited for; matrix products, arithmetic and copies ran while one was open for 7% of the time, Pallas kernels for 0%

commit v1 on v0

v1 whole, which is shorter than its diff:
```python
import functools

import jax
import jax.numpy as jnp
import numpy as np
from jax import lax
from jax.experimental import pallas as pl
from jax.experimental.pallas import tpu as pltpu
from jax.sharding import PartitionSpec as P

NOPE = 128
ROPE = 64
VDIM = 128
EPS = 1e-06
SEQ = 64
MESH = pl.DeviceIdType.MESH
F32 = jnp.float32
BF16 = jnp.bfloat16


def rotation_tables(share):
    row = np.arange(2 * SEQ)
    position = (row // (2 * share)) * share + row % share
    lane = np.arange(128)
    freq = np.exp(-np.log(10000.0) * (lane % 32) / 32.0)
    angle = position[:, None] * freq[None, :]
    sign = np.where(lane % 64 < 32, -1.0, 1.0)
    return np.cos(angle).astype(np.float32), (np.sin(angle) * sign).astype(np.float32)


def mm(a, b):
    return jnp.dot(a.astype(BF16), b.astype(BF16), preferred_element_type=F32)


def mm_nt(a, b):
    return lax.dot_general(
        a.astype(BF16), b.astype(BF16), (((1,), (1,)), ((), ())), preferred_element_type=F32
    )


def mm_tn(a, b):
    return lax.dot_general(
        a.astype(BF16), b.astype(BF16), (((0,), (0,)), ((), ())), preferred_element_type=F32
    )


def swap_halves(v):
    lane = lax.broadcasted_iota(jnp.int32, v.shape, 1)
    return jnp.where(lane % 64 < 32, pltpu.roll(v, 96, axis=1), pltpu.roll(v, 32, axis=1))


def kernel(
    sizes,
    x_ref,
    top_ref,
    gain_ref,
    wq_ref,
    wlat_ref,
    cgain_ref,
    wexp_ref,
    wout_ref,
    cos_ref,
    sin_ref,
    dx_out,
    gain_out,
    q_out,
    lat_out,
    lg_out,
    exp_out,
    o_out,
    wg,
    gg,
    xs,
    up,
    part,
    prec,
    dxs,
    rbuf,
    ysend,
    yrecv,
    tot,
    tsend,
    trecv,
    agy_s,
    agy_r,
    ag_s,
    ag_r,
    hop_s,
    hop_r,
    ua_s,
    ua_r,
    tr_s,
    tr_r,
    rs_s,
    rs_r,
    rsy_s,
    rsy_r,
    tg_s,
    tg_r,
):
    sections, nz, nt, width, rank = sizes
    share = SEQ // nt
    rows = 2 * share
    tokens = 2 * SEQ
    cg_at = 512 + rank
    full = cg_at + 128
    pipe = lax.axis_index("pipe")
    dp = lax.axis_index("dp")
    t = lax.axis_index("tensor")
    yl = lax.div(dp, nz)
    z = lax.rem(dp, nz)
    z_right = yl * nz + lax.rem(z + 1, nz)
    z_left = yl * nz + lax.rem(z + nz - 1, nz)
    y_mate = (1 - yl) * nz + z
    others = [k for k in (4, 3, 5, 2, 6, 1, 7) if k < nt]
    arms = (nz // 2, nz - 1 - nz // 2)
    z_to = (z_right, z_left)

    barrier = pltpu.get_barrier_semaphore()

    def greet(where):
        pl.semaphore_signal(barrier, inc=1, device_id=where, device_id_type=MESH)

    greet({"dp": z_right})
    greet({"dp": z_left})
    greet({"dp": y_mate})
    greet({"pipe": lax.rem(pipe + 1, sections)})
    greet({"pipe": lax.rem(pipe + sections - 1, sections)})
    for k in others:
        greet({"tensor": lax.rem(t + k, nt)})

    def block(owner, half=None):
        if half is None:
            return pl.ds(pl.multiple_of(owner * 32, 32), 32)
        return pl.ds(pl.multiple_of(owner * 32 + half * 16, 16), 16)

    own = block(dp)
    wg[own, 0:128] = wout_ref[...].astype(F32).T.astype(BF16)
    wg[block(dp, 0), 128:256] = wexp_ref[:, 0:128]
    wg[block(dp, 1), 128:256] = wexp_ref[:, 128:256]
    wg[own, 256:384] = wq_ref[:, 0:128]
    wg[own, 384:512] = jnp.concatenate(
        [wq_ref[:, 128:192].astype(F32), wlat_ref[:, rank : rank + 64].astype(F32)], axis=1
    ).astype(BF16)
    wg[own, 512:cg_at] = wlat_ref[:, 0:rank]
    lane = lax.broadcasted_iota(jnp.int32, (32, 128), 1)
    line = lax.broadcasted_iota(jnp.int32, (32, 128), 0)
    gain_tile = jnp.concatenate([gain_ref[...].astype(F32)] * 4, axis=1)
    gain_tile = jnp.broadcast_to(gain_tile, (32, 128))
    cgain_tile = jnp.concatenate([cgain_ref[...].astype(F32)] * 8, axis=1)
    cgain_tile = jnp.broadcast_to(cgain_tile, (32, 128))
    placed = jnp.where(
        jnp.logical_and(line == 0, lane // 32 == lax.rem(dp, 4)),
        gain_tile,
        jnp.where(jnp.logical_and(line == 1, lane // 16 == lax.rem(dp, 8)), cgain_tile, 0.0),
    )
    wg[own, cg_at:full] = placed.astype(BF16)

    x32 = x_ref[...].astype(F32)
    for i in range(nt):
        xs[i, 0:share, :] = x32[0, i * share : (i + 1) * share, :]
        xs[i, share:rows, :] = x32[1, i * share : (i + 1) * share, :]

    pl.semaphore_wait(barrier, 5 + len(others))

    def mate_copy(half, owner):
        ref = wg.at[block(owner, half), :]
        return pltpu.make_async_remote_copy(
            ref, ref, agy_s.at[half], agy_r.at[half], device_id={"dp": y_mate}, device_id_type=MESH
        )

    def ring_copy(arm, step, other, half, away):
        shift = step + away
        at = lax.rem(z + nz - shift, nz) if arm == 0 else lax.rem(z + shift, nz)
        line_at = (1 - yl) if other else yl
        ref = wg.at[block(line_at * nz + at, half), :]
        return pltpu.make_async_remote_copy(
            ref,
            ref,
            ag_s.at[arm, step, 2 * other + half],
            ag_r.at[arm, step, 2 * other + half],
            device_id={"dp": z_to[arm]},
            device_id_type=MESH,
        )

    for half in range(2):
        mate_copy(half, dp).start()
        for arm in range(2):
            if arms[arm] > 0:
                ring_copy(arm, 0, 0, half, 0).start()
    for half in range(2):
        mate_copy(half, y_mate).wait_recv()
        for arm in range(2):
            if arms[arm] > 0:
                ring_copy(arm, 0, 1, half, 0).start()
    for step in range(1, arms[0] + 1):
        for other in range(2):
            for half in range(2):
                for arm in range(2):
                    if step <= arms[arm]:
                        ring_copy(arm, step - 1, other, half, 1).wait_recv()
                    if step < arms[arm]:
                        ring_copy(arm, step, other, half, 0).start()

    def gathered_rows(line_at, tiles, per):
        pieces = []
        for tile in range(tiles):
            total = None
            for i in range(per):
                owner = tile * per + i
                value = wg[owner * 32 : owner * 32 + 16, cg_at:full].astype(F32)
                value = value[line_at : line_at + 1, :]
                total = value if total is None else total + value
            pieces.append(total)
        return jnp.concatenate(pieces, axis=1)

    gain = gathered_rows(0, width // 128, 4)
    cgain = gathered_rows(1, rank // 128, 8)
    cosine = cos_ref[...]
    sine = sin_ref[...]

    xf = xs[...].reshape(tokens, width)
    scale_x = lax.rsqrt(jnp.mean(xf * xf, axis=-1, keepdims=True) + EPS)
    rounded = (xf * scale_x * gain).astype(BF16)
    projected = mm(rounded, wg[:, 256:cg_at])
    q_nope = projected[:, 0:128]
    ropes = projected[:, 128:256]
    latent = projected[:, 256:]
    scale_c = lax.rsqrt(jnp.mean(latent * latent, axis=-1, keepdims=True) + EPS)
    latent_hat = latent * scale_c
    compressed = (latent_hat * cgain).astype(BF16)
    ropes = ropes * cosine + swap_halves(ropes) * sine
    wexp = wg[:, 128:256].reshape(2 * nz, 2, 16, 128)
    wexp = jnp.concatenate(
        [wexp[:, 0].reshape(rank, 128), wexp[:, 1].reshape(rank, 128)], axis=1
    )
    expanded = mm(compressed, wexp)
    values = expanded[:, 128:256].astype(BF16)
    lane2 = lax.broadcasted_iota(jnp.int32, (tokens, 128), 1)
    row2 = lax.broadcasted_iota(jnp.int32, (tokens, 128), 0)
    queries = jnp.concatenate([q_nope, jnp.where(lane2 < 64, ropes, 0.0)], axis=1).astype(BF16)
    keys = jnp.concatenate(
        [expanded[:, 0:128], jnp.where(lane2 < 64, pltpu.roll(ropes, 64, axis=1), 0.0)], axis=1
    ).astype(BF16)
    score_scale = (NOPE + ROPE) ** (-0.5)
    scores = mm_nt(queries, keys) * score_scale
    row_position = (row2 // rows) * share + row2 % share
    key_position = (lane2 // rows) * share + lane2 % share
    same = (row2 // share) % 2 == (lane2 // share) % 2
    keep = jnp.logical_and(same, row_position >= key_position)
    scores = jnp.where(keep, scores, -1e30)
    powers = jnp.exp(scores - jnp.max(scores, axis=-1, keepdims=True))
    weights = powers / jnp.sum(powers, axis=-1, keepdims=True)
    weights16 = weights.astype(BF16)
    mixed = mm(weights16, values).astype(BF16)

    def hop_copy(to):
        return pltpu.make_async_remote_copy(
            dxs, up.at[t], hop_s, hop_r, device_id={"pipe": to}, device_id_type=MESH
        )

    def share_copy(k, at):
        ref = up.at[at]
        return pltpu.make_async_remote_copy(
            ref,
            ref,
            ua_s.at[k],
            ua_r.at[k],
            device_id={"tensor": lax.rem(t + k, nt)},
            device_id_type=MESH,
        )

    @pl.when(pipe == sections - 1)
    def _():
        top = top_ref[...].astype(F32)
        for i in range(nt):
            up[i] = jnp.concatenate(
                [top[0, i * share : (i + 1) * share, :], top[1, i * share : (i + 1) * share, :]],
                axis=0,
            ).astype(BF16)

    @pl.when(pipe < sections - 1)
    def _():
        hop_copy(pipe).wait_recv()
        for k in others:
            share_copy(k, t).start()
        for k in others:
            share_copy(k, lax.rem(t + nt - k, nt)).wait_recv()
        for k in others:
            share_copy(k, t).wait_send()

    upstream = up[...].reshape(tokens, width)
    d_mixed = mm(upstream, wg[:, 0:128]).astype(BF16)
    d_weights = mm_nt(d_mixed, values).astype(BF16).astype(F32)
    d_values = mm_tn(weights16, d_mixed).astype(BF16)
    d_scores = weights * (d_weights - jnp.sum(weights * d_weights, axis=-1, keepdims=True))
    d_scores = (d_scores * score_scale).astype(BF16)
    d_queries = mm(d_scores, keys)
    d_keys = mm_tn(d_scores, queries)
    d_ropes = d_queries[:, 128:256] + pltpu.roll(d_keys[:, 128:256], 64, axis=1)
    d_ropes = d_ropes * cosine - swap_halves(d_ropes) * sine
    d_expanded = jnp.concatenate([d_keys[:, 0:128].astype(BF16), d_values], axis=1)
    d_compressed = mm_nt(d_expanded, wexp).astype(BF16).astype(F32)
    d_cgain = jnp.sum(d_compressed * latent_hat, axis=0, keepdims=True)
    d_hat = d_compressed * cgain
    d_latent = scale_c * (d_hat - latent_hat * jnp.mean(d_hat * latent_hat, axis=-1, keepdims=True))
    d_projected = jnp.concatenate(
        [d_queries[:, 0:128].astype(BF16), d_ropes.astype(BF16), d_latent.astype(BF16)], axis=1
    )
    d_rounded = mm_nt(d_projected, wg[:, 256:cg_at]).astype(BF16)
    part[...] = d_rounded.reshape(nt, rows, width)

    def spread_copy(k):
        return pltpu.make_async_remote_copy(
            part.at[lax.rem(t + k, nt)],
            prec.at[k],
            tr_s.at[k],
            tr_r.at[k],
            device_id={"tensor": lax.rem(t + k, nt)},
            device_id_type=MESH,
        )

    for k in others:
        spread_copy(k).start()

    gg[:, 256:cg_at] = mm_tn(rounded, d_projected).astype(BF16)
    gg[:, 0:128] = mm_tn(upstream, mixed).astype(BF16)
    g_exp = mm_tn(compressed, d_expanded).astype(BF16)
    for owner in range(2 * nz):
        gg[owner * 32 : owner * 32 + 16, 128:256] = g_exp[owner * 16 : owner * 16 + 16, 0:128]
        gg[owner * 32 + 16 : owner * 32 + 32, 128:256] = g_exp[
            owner * 16 : owner * 16 + 16, 128:256
        ]

    for k in others:
        spread_copy(k).wait_recv()
    total = part[t].astype(F32)
    for k in others:
        total = total + prec[k].astype(F32)

    x_own = xs[t]
    scale_own = lax.rsqrt(jnp.mean(x_own * x_own, axis=-1, keepdims=True) + EPS)
    hat_own = x_own * scale_own
    d_gain = jnp.sum(total * hat_own, axis=0, keepdims=True)
    d_own = total * gain
    d_x = scale_own * (d_own - hat_own * jnp.mean(d_own * hat_own, axis=-1, keepdims=True))
    d_x = (up[t].astype(F32) + d_x).astype(BF16)
    dxs[...] = d_x

    @pl.when(pipe > 0)
    def _():
        hop_copy(pipe - 1).start()

    d_x32 = d_x.astype(F32)
    dx_out[0] = d_x32[0:share, :].astype(BF16)
    dx_out[1] = d_x32[share:rows, :].astype(BF16)

    for owner in range(2 * nz):
        g_tile = d_gain[:, (owner // 4) * 128 : (owner // 4) * 128 + 128]
        c_tile = d_cgain[:, (owner // 8) * 128 : (owner // 8) * 128 + 128]
        gg[owner * 32 : owner * 32 + 32, cg_at:full] = jnp.where(
            line == 0, g_tile, jnp.where(line == 1, c_tile, 0.0)
        ).astype(BF16)

    def ring_target(arm, step):
        if arm == 0:
            return lax.rem(z + arms[0] - step, nz)
        return lax.rem(z + nz - (arms[1] - step), nz)

    def arrived(arm, step, own_line, half):
        return rbuf.at[arm, step, own_line, half * 16 : half * 16 + 16, :]

    def sum_copy(arm, step, own_line, half):
        if step == 0:
            line_at = yl if own_line else 1 - yl
            source = gg.at[block(line_at * nz + ring_target(arm, 0), half), :]
        else:
            source = arrived(arm, step - 1, own_line, half)
        return pltpu.make_async_remote_copy(
            source,
            arrived(arm, step, own_line, half),
            rs_s.at[arm, step, 2 * own_line + half],
            rs_r.at[arm, step, 2 * own_line + half],
            device_id={"dp": z_to[arm]},
            device_id_type=MESH,
        )

    def y_copy(half):
        return pltpu.make_async_remote_copy(
            ysend.at[half],
            yrecv.at[half],
            rsy_s.at[half],
            rsy_r.at[half],
            device_id={"dp": y_mate},
            device_id_type=MESH,
        )

    for step in range(arms[0] + 1):
        for own_line in range(2):
            line_at = yl if own_line else 1 - yl
            for half in range(2):
                for arm in range(2):
                    if 0 < step <= arms[arm]:
                        sum_copy(arm, step - 1, own_line, half).wait_recv()
                    if 0 < step < arms[arm]:
                        here = block(line_at * nz + ring_target(arm, step), half)
                        held = arrived(arm, step - 1, own_line, half)
                        held[...] = (held[...].astype(F32) + gg[here, :].astype(F32)).astype(BF16)
                    if step < arms[arm]:
                        sum_copy(arm, step, own_line, half).start()
                if step == arms[0]:
                    value = gg[block(line_at * nz + z, half), :].astype(F32)
                    for arm in range(2):
                        if arms[arm] > 0:
                            value = value + arrived(arm, arms[arm] - 1, own_line, half)[...].astype(F32)
                    if own_line:
                        tot[half] = value
                    else:
                        ysend[half] = value.astype(BF16)
                        y_copy(half).start()

    def tensor_copy(k, half):
        return pltpu.make_async_remote_copy(
            tsend.at[half],
            trecv.at[k, half],
            tg_s.at[k, half],
            tg_r.at[k, half],
            device_id={"tensor": lax.rem(t + k, nt)},
            device_id_type=MESH,
        )

    for half in range(2):
        y_copy(half).wait_recv()
        value = tot[half] + yrecv[half].astype(F32)
        tot[half] = value
        tsend[half] = value[:, 384:].astype(BF16)
        for k in others:
            tensor_copy(k, half).start()

    for half in range(2):
        at = half * 16
        value = tot[half]
        o_rows = value[:, 0:128]
        q_out[at : at + 16, 0:128] = value[:, 256:384]
        q_out[at : at + 16, 128:192] = value[:, 384:448]
        exp_out[:, half * 128 : half * 128 + 128] = value[:, 128:256]
        tot[half, :, 0:128] = o_rows
    o_out[...] = jnp.concatenate([tot[0][:, 0:128], tot[1][:, 0:128]], axis=0).T

    for half in range(2):
        at = half * 16
        for k in others:
            tensor_copy(k, half).wait_recv()
        value = tsend[half].astype(F32)
        for k in others:
            value = value + trecv[k, half].astype(F32)
        lat_out[at : at + 16, 0:rank] = value[:, 128 : 128 + rank]
        lat_out[at : at + 16, rank : rank + 64] = value[:, 64:128]
        if half == 0:
            g_row = value[0:1, 128 + rank :]
            c_row = value[1:2, 128 + rank :]
            g_sum = jnp.zeros((1, 32), F32)
            for k in range(4):
                g_sum = g_sum + jnp.where(lax.rem(dp, 4) == k, g_row[:, 32 * k : 32 * k + 32], 0.0)
            c_sum = jnp.zeros((1, 16), F32)
            for k in range(8):
                c_sum = c_sum + jnp.where(lax.rem(dp, 8) == k, c_row[:, 16 * k : 16 * k + 16], 0.0)
            gain_out[...] = g_sum
            lg_out[...] = c_sum

    for half in range(2):
        mate_copy(half, dp).wait_send()
        y_copy(half).wait_send()
        for k in others:
            tensor_copy(k, half).wait_send()
        for other in range(2):
            for arm in range(2):
                for step in range(arms[arm]):
                    ring_copy(arm, step, other, half, 0).wait_send()
                    sum_copy(arm, step, other, half).wait_send()
    for k in others:
        spread_copy(k).wait_send()

    @pl.when(pipe > 0)
    def _():
        hop_copy(pipe - 1).wait_send()


def shards(saved, top_grad, gain, w_query, w_latent, compressed_gain, expand_weight, w_output):
    sections = lax.axis_size("pipe")
    nz = lax.axis_size("dp") // 2
    nt = lax.axis_size("tensor")
    width = saved.shape[3]
    rank = w_latent.shape[2] - ROPE
    share = SEQ // nt
    rows = 2 * share
    full = 640 + rank
    steps = nz // 2
    cosine, sine = rotation_tables(share)
    vmem = pl.BlockSpec(memory_space=pltpu.VMEM)
    dma = pltpu.SemaphoreType.DMA
    outs = pl.pallas_call(
        functools.partial(kernel, (sections, nz, nt, width, rank)),
        out_shape=(
            jax.ShapeDtypeStruct((2, share, width), BF16),
            jax.ShapeDtypeStruct((1, 32), F32),
            jax.ShapeDtypeStruct((32, NOPE + ROPE), F32),
            jax.ShapeDtypeStruct((32, rank + ROPE), F32),
            jax.ShapeDtypeStruct((1, 16), F32),
            jax.ShapeDtypeStruct((16, NOPE + VDIM), F32),
            jax.ShapeDtypeStruct((VDIM, 32), F32),
        ),
        in_specs=[vmem] * 10,
        out_specs=(vmem,) * 7,
        scratch_shapes=[
            pltpu.VMEM((width, full), BF16),
            pltpu.VMEM((width, full), BF16),
            pltpu.VMEM((nt, rows, width), F32),
            pltpu.VMEM((nt, rows, width), BF16),
            pltpu.VMEM((nt, rows, width), BF16),
            pltpu.VMEM((nt, rows, width), BF16),
            pltpu.VMEM((rows, width), BF16),
            pltpu.VMEM((2, steps, 2, 32, full), BF16),
            pltpu.VMEM((2, 16, full), BF16),
            pltpu.VMEM((2, 16, full), BF16),
            pltpu.VMEM((2, 16, full), F32),
            pltpu.VMEM((2, 16, full - 384), BF16),
            pltpu.VMEM((nt, 2, 16, full - 384), BF16),
            dma((2,)),
            dma((2,)),
            dma((2, steps, 4)),
            dma((2, steps, 4)),
            dma,
            dma,
            dma((nt,)),
            dma((nt,)),
            dma((nt,)),
            dma((nt,)),
            dma((2, steps, 4)),
            dma((2, steps, 4)),
            dma((2,)),
            dma((2,)),
            dma((nt, 2)),
            dma((nt, 2)),
        ],
        compiler_params=pltpu.CompilerParams(
            collective_id=0, has_side_effects=True, vmem_limit_bytes=48 * 1024 * 1024
        ),
        name="relay",
    )(
        saved[0],
        top_grad,
        gain,
        w_query[0],
        w_latent[0],
        compressed_gain,
        expand_weight[0],
        w_output[0],
        jnp.asarray(cosine),
        jnp.asarray(sine),
    )
    dx, g_gain, g_q, g_lat, g_lg, g_exp, g_out = outs
    return dx[None], g_gain, g_q[None], g_lat[None], g_lg, g_exp[None], g_out[None]


def solution(mesh):
    in_specs = (
        P("pipe", None, "dp", None),
        P(None, "dp", None),
        P("pipe", "dp"),
        P("pipe", "dp", "tensor"),
        P("pipe", "dp", None),
        P("pipe", "dp"),
        P("pipe", "dp", "tensor"),
        P("pipe", "tensor", "dp"),
    )
    out_specs = (
        P("pipe", None, ("dp", "tensor"), None),
        P("pipe", "dp"),
        P("pipe", "dp", "tensor"),
        P("pipe", "dp", None),
        P("pipe", "dp"),
        P("pipe", "dp", "tensor"),
        P("pipe", "tensor", "dp"),
    )
    return jax.shard_map(shards, mesh=mesh, in_specs=in_specs, out_specs=out_specs, check_vma=False)
```

time: 680 us -> 152 us (0.22)
  waiting for transfers between devices: 332 us -> 0 us
  Pallas kernels: 0 us -> 141 us
  blocking collectives: 116 us -> 0 us
  starting transfers between devices: 88.3 us -> 0 us
  local copies, waits for them, and re-layouts: 53.7 us -> 9.94 us
  other arithmetic: 37.8 us -> 0 us
  matrix products: 33.3 us -> 0 us
  between operations: 16.2 us -> 0.7 us
    unnamed x3 -> x0, waiting for transfers between devices: 233 us -> none
    pallas_call x0 -> x1, Pallas kernels: none -> 141 us  [shards(): pl.pallas_call(functools.partial(kernel, (sections, nz, nt, width, rank))...]
    all_gather x2 -> x0, blocking collectives: 116 us -> none  [the longest x1 66.4 us: side_by_side(): lax.all_gather(both, axis, axis=dim, tiled=True)]
    all_to_all x8 -> x0, starting transfers between devices: 83 us -> none  [from_everyone(): lax.all_to_all(jnp.broadcast_to(x[None], (length, *x.shape)), axis, 0, 0,...]
    all_to_all x8 -> x0, waiting for transfers between devices: 54.4 us -> none  [from_everyone(): lax.all_to_all(jnp.broadcast_to(x[None], (length, *x.shape)), axis, 0, 0,...]
    ppermute x4 -> x0, waiting for transfers between devices: 39.1 us -> none  [passed_along(): lax.ppermute(value, axis, [(source, source + steps) for source in range(f...]
    dot_general x64 -> x0, matrix products: 33.3 us -> none  [the longest x8 10.5 us: branch(): jnp.dot(rounded, w_q, preferred_element_type=jnp.float32)]
    reduce_sum x26 -> x0, other arithmetic: 15.8 us -> none  [the longest x8 9.04 us: taken_together(): return jnp.sum(everything.astype(jnp.float32), axis=0)]
  transfers between devices with their start and end apart: 14 -> 0, of which waited for: 13 -> 0; matrix products, arithmetic and copies ran while one was open for 7% -> 0% of each run, Pallas kernels for 0% -> 0%
where the time goes in v1:
time: 152 us
  Pallas kernels  141 us (93%)
  local copies, waits for them, and re-layouts  9.94 us (7%)
    pallas_call x1, Pallas kernels, shards(): pl.pallas_call(functools.partial(kernel, (sections, nz, nt, width, rank))...  141 us
    unnamed x26, local copies, waits for them, and re-layouts  9.94 us

profile of v1, /device:TPU:1, one launch (start us, length us, event | category | flops | bytes accessed | tf_op | source)
XLA Modules:
  0.0 151.9 jit_solution(12634265759851841493)
XLA Ops:
  0.6 0.0 copy-start.4
  0.6 0.0 copy-start.6
  0.7 0.8 copy.17
  1.5 0.0 copy-start.7
  1.5 0.0 copy-start.8
  1.5 0.0 copy-done.4
  1.5 0.0 copy-done.6
  1.5 0.6 copy-done.7
  2.1 0.0 copy-done.8
  2.2 0.0 copy-start
  2.2 0.9 copy-done
  3.1 0.0 copy-start.1
  3.1 0.9 copy-done.1
  4.1 0.0 copy-start.2
  4.1 0.8 copy-done.2
  4.9 0.0 copy-start.3
  4.9 0.8 copy-done.3
  5.7 0.0 copy-start.5
  5.7 0.7 copy-done.5
  6.5 141.2 %relay.1 = (bf16[2,8,1024]{2,1,0:T(8,128)(2,1)S(1)}, f32[1,32]{1,0:T(1,128)S(1)}, f32[32,192]{1,0:T(8,128)S(1)}, f32[32,576]{1,0:T(8,128)S(1)}, f32[1,16]{1,0:T(...) custom-call(bf16[2,64,1024]{2,1,0:T(8,128)(2,1)S(1)} %bitcast.10, bf16[2,64,1024]{2,1,0:T(8,128)(2,1)S(1)} %copy-done.1, ...), custom_call_target="tpu_custom_call" | custom-call | tf_op jit(solution)/shard_map/relay/pallas_call | solution.py:502
  147.7 0.7 copy.18
  148.4 0.6 copy.25
  149.0 0.5 copy.26
  149.5 0.6 copy.27
  150.1 0.6 copy.28
  150.8 0.5 copy.29
  151.3 0.6 copy.30
Async XLA Ops:
  0.6 0.9 copy-start.4
  0.6 0.9 copy-start.6
  1.5 0.7 copy-start.7
  1.5 0.7 copy-start.8
  2.2 0.9 copy-start
  3.1 0.9 copy-start.1
  4.1 0.8 copy-start.2
  4.9 0.8 copy-start.3
  5.7 0.7 copy-start.5
